TPU v7x, 512 devices: a whole 4x8x8 slice. The times are simulated.
512 devices in a mesh: tok: 8 (over x, core), voc: 64 (over z, y).
Axes of the slice: x: 4, y: 8, z: 8, core: 2. Of those that a mesh axis runs over, the one named last changes fastest.
Arguments:
- hidden: bfloat16 [1024, 4608], P(('tok', 'voc')), may hold values from -6 to 6
- norm_gain: float32 [4608], replicated, may hold values from 0.25 to 1.75
- head_weight: bfloat16 [262144, 4608], P(('tok', 'voc')), may hold values from -0.26367188 to 0.26367188
- targets: int32 [1024], replicated, may hold values from 0 to 262143
- lengths: int32 [32], replicated, may hold values from 1 to 32
Outputs:
- token_loss: float32 [1024], P(('tok', 'voc'))
- mean_loss: float32 [], replicated
All inputs are finite; a program needn't handle non-finite values.
Results may differ from a plain program's by a relative error of at most 0.00051.
Values may be sent and summed in bfloat16 or wider, within the bound.
No kernel may reach another device: no remote copies, remote signals or barrier semaphores. Data moves between devices by JAX's collectives and lax.ppermute only.
A program may use at most 64 MiB of HBM per device.

v0:
```python
import functools
import jax
import jax.numpy as jnp
from jax import lax
from jax.sharding import Mesh
from jax.sharding import PartitionSpec as P

WINDOW = 32
TOK_VOC = ("tok_0", "tok_1", "voc_0", "voc_1")
VOC = ("voc_0", "voc_1")
TOK = ("tok_0", "tok_1")


def laid_out(parts, dim):
    lengths = list(parts.shape[1:])
    lengths[dim] *= parts.shape[0]
    return jnp.moveaxis(parts, 0, dim).reshape(lengths)


def gather_in_order(value, axes, turns):
    parts = value[None]
    for k in turns:
        parts = lax.all_gather(parts, axes[k], axis=0, tiled=True)
    held = [lax.axis_size(axes[k]) for k in reversed(turns)]
    parts = parts.reshape(*held, *value.shape)
    turned = sorted(range(len(turns)), key=lambda place: turns[len(turns) - 1 - place])
    return parts.transpose(*turned, *range(len(turns), parts.ndim)).reshape(-1, *value.shape)


def gather_axes(value, axes, turns, dim):
    return laid_out(gather_in_order(value, axes, turns), dim)


def over_axes(value, axes):
    return functools.reduce(lax.psum, axes, value)


def body(hidden, norm_gain, head_weight, targets, lengths):
    own_rows = hidden.shape[0]
    vocab_rows = head_weight.shape[0]
    everyone = lax.axis_size(TOK_VOC)
    whole = own_rows * everyone
    window = WINDOW
    me = lax.axis_index(TOK_VOC)
    values = hidden.astype(jnp.float32)
    meansq = jnp.mean(values * values, axis=1, keepdims=True)
    normed = (values * lax.rsqrt(meansq + 1e-06) * norm_gain[None, :]).astype(jnp.bfloat16)
    offset = me * vocab_rows
    column = jnp.arange(vocab_rows, dtype=jnp.int32)
    grouped = gather_axes(normed, VOC, (0, 1), 0)
    logits = lax.dot_general(
        lax.all_gather(grouped, TOK, axis=0, tiled=True),
        head_weight,
        (((1,), (1,)), ((), ())),
        preferred_element_type=jnp.float32,
    )
    capped = 30.0 * jnp.tanh(logits / 30.0)
    expsum = jnp.sum(jnp.exp(capped), axis=1)
    wanted = targets - offset
    match = column[None, :] == wanted[:, None]
    picked = jnp.sum(jnp.where(match, capped, jnp.zeros_like(capped)), axis=1)
    stats = jnp.stack([expsum, picked])
    position = jnp.arange(window, dtype=jnp.int32)
    live_all = (position[None, :] < lengths[:, None]).astype(jnp.float32).reshape(whole)
    count = jnp.sum(lengths.astype(jnp.float32))
    totals = over_axes(stats, TOK_VOC)
    loss_all = live_all * (jnp.log(totals[0]) - totals[1])
    mean_loss = jnp.sum(loss_all) / count
    token_loss = lax.dynamic_slice_in_dim(loss_all, me * own_rows, own_rows, 0)
    return (token_loss, mean_loss)


def solution(mesh):
    split = Mesh(mesh.devices.reshape(4, 2, 8, 8), ("tok_0", "tok_1", "voc_0", "voc_1"))
    in_specs = (P(TOK_VOC, None), P(), P(TOK_VOC, None), P(), P())
    out_specs = (P(TOK_VOC), P())
    return jax.shard_map(body, mesh=split, in_specs=in_specs, out_specs=out_specs, check_vma=False)
```

profile of v0, /device:TPU:2, one launch (start us, length us, event | category | flops | bytes accessed | tf_op | source)
XLA Modules:
  0.0 209.9 jit_solution(8907988233021880840)
XLA Ops:
  7.2 0.0 all-gather.5.cloned.1.call-start
  7.2 0.9 fusion
  8.1 0.8 fusion.3
  8.9 33.0 %all-gather.1 = bf16[8,2,4608]{2,1,0:T(2,128)(2,1)} all-gather(bf16[1,2,4608]{2,1,0:T(2,128)(2,1)S(1)} %fusion.3), channel_id=2, replica_groups=mesh['tok_0'=4,'tok_1'=2,'voc_0'=8,'voc_1'=8] {'voc_0'}, dimensions={0}, use_global_device_ids=true | all-gather | bytes 165888 | tf_op jit(solution)/shard_map/all_gather | solution.py:23
  41.9 0.0 all-gather.5.cloned.1.call-update
  42.0 0.0 all-gather.7.cloned.1.call-start
  42.0 39.3 %all-gather.5.cloned.1.call-done = bf16[64,2,4608]{2,1,0:T(2,128)(2,1)} async-done(((bf16[8,2,4608]{2,1,0:T(2,128)(2,1)}), bf16[64,2,4608]{2,1,0:T(2,128)(2,1)}) %all-gather.5.cloned.1.call-update) | async-done | bytes 1179664 | tf_op jit(solution)/shard_map/all_gather | solution.py:23
  81.3 2.1 copy.11
  83.4 0.0 copy-start.1
  83.4 0.0 copy-start
  83.4 1.3 reshape_reshape.3
  84.7 0.0 all-gather.7.cloned.1.call-update
  84.7 0.1 iota_compare_fusion.1
  84.8 0.1 lt.34
  84.9 0.1 lt.32
  85.0 0.7 convert_reduce_fusion
  85.7 56.9 %all-gather.7.cloned.1.call-done = bf16[1024,4608]{1,0:T(8,128)(2,1)} async-done(((bf16[128,4608]{1,0:T(8,128)(2,1)}), bf16[1024,4608]{1,0:T(8,128)(2,1)}) %all-gather.7.cloned.1.call-update) | async-done | bytes 9437200 | tf_op jit(solution)/shard_map/all_gather | solution.py:52
  142.6 9.5 %exponential_reduce_fusion = (f32[1024]{0:T(1024)S(1)}, f32[1024]{0:T(1024)S(1)}) fusion(s32[1024]{0:T(1024)S(1)} %broadcast_subtract_fusion, bf16[1024,4608]{1,0:T(8,128)(2,1)} %all-gather.7.cloned.1.call-done, bf16[512,4608]{1,0:T(8,128)(2,1)} %param.7), kind=kOutput, calls=%fused_computation.2 | convolution fusion | flops 4834981888 | bytes 14168064 | tf_op jit(solution)/shard_map/dot_general | solution.py:51
  152.1 9.1 %psum.28 = f32[2,1024]{1,0:T(2,128)S(1)} all-reduce(f32[2,1024]{1,0:T(2,128)S(1)} %pad_maximum_fusion), channel_id=1, replica_groups=mesh['tok_0'=4,'tok_1'=2,'voc_0'=8,'voc_1'=8] {'tok_0'}, use_global_device_ids=true, to_apply=%region_3.4 | all-reduce | flops 2048 | bytes 16384 | tf_op jit(solution)/shard_map/psum | solution.py:35
  161.2 2.5 %psum.29 = f32[2,1024]{1,0:T(2,128)S(1)} all-reduce(f32[2,1024]{1,0:T(2,128)S(1)} %psum.28), channel_id=1, replica_groups=mesh['tok_0'=4,'tok_1'=2,'voc_0'=8,'voc_1'=8] {'tok_1'}, use_global_device_ids=true, to_apply=%region_4.5 | all-reduce | flops 2048 | bytes 16384 | tf_op jit(solution)/shard_map/psum | solution.py:35
  163.7 18.3 %psum.30 = f32[2,1024]{1,0:T(2,128)S(1)} all-reduce(f32[2,1024]{1,0:T(2,128)S(1)} %psum.29), channel_id=1, replica_groups=mesh['tok_0'=4,'tok_1'=2,'voc_0'=8,'voc_1'=8] {'voc_0'}, use_global_device_ids=true, to_apply=%region_5.6 | all-reduce | flops 2048 | bytes 16384 | tf_op jit(solution)/shard_map/psum | solution.py:35
  182.1 17.2 %psum.31 = f32[2,1024]{1,0:T(2,128)S(1)} all-reduce(f32[2,1024]{1,0:T(2,128)S(1)} %psum.30), channel_id=1, replica_groups=mesh['tok_0'=4,'tok_1'=2,'voc_0'=8,'voc_1'=8] {'voc_1'}, use_global_device_ids=true, to_apply=%region_6.7 | all-reduce | flops 2048 | bytes 16384 | tf_op jit(solution)/shard_map/psum | solution.py:35
  199.3 0.6 select_reduce_fusion.1
  199.9 0.6 dynamic_slice.3
  (6 shorter events, 0.0 us)
Async XLA Ops:
  7.2 74.1 %all-gather.5.cloned.1.call-start = ((), (), s32[]{:S(2)}) async-start(), calls=%async_computation | async-start | bytes 1327104 | tf_op jit(solution)/shard_map/all_gather | solution.py:23
  42.0 100.6 %all-gather.7.cloned.1.call-start = ((), (), s32[]{:S(2)}) async-start(), calls=%async_computation.1 | async-start | bytes 10616832 | tf_op jit(solution)/shard_map/all_gather | solution.py:52
  83.4 1.3 copy-start.1
  83.4 2.3 %copy-start = (s32[1024]{0:T(1024)S(1)}, s32[1024]{0:T(1024)}, u32[]{:S(2)}) copy-start(s32[1024]{0:T(1024)} %param.8) | copy-start | bytes 12292
Sparse Core Ops, SparseCore 0:
  42.1 39.1 all-gather.4
  84.8 57.7 all-gather.6
where the time goes:
time: 210 us
  waiting for transfers between devices  96.3 us (46%)
  blocking collectives  80.2 us (38%)
  between operations  16.6 us (8%)
  matrix products  9.45 us (4%)
  local copies, waits for them, and re-layouts  4.13 us (2%)
  other arithmetic  3.11 us (1%)
    all_gather x1, waiting for transfers between devices, body(): lax.all_gather(grouped, TOK, axis=0, tiled=True)  56.9 us
    psum x4, blocking collectives, over_axes(): return functools.reduce(lax.psum, axes, value)  47.2 us
    all_gather x1, waiting for transfers between devices, gather_in_order(): parts = lax.all_gather(parts, axes[k], axis=0, tiled=True)  39.3 us
    all_gather x1, blocking collectives, gather_in_order(): parts = lax.all_gather(parts, axes[k], axis=0, tiled=True)  33 us
    dot_general x1, matrix products, body(): lax.dot_general(lax.all_gather(grouped, TOK, axis=0, tiled=True), head_we...  9.45 us
  transfers between devices with their start and end apart: 2, of which 2 were waited for; matrix products, arithmetic and copies ran while one was open for 0% of the time, Pallas kernels for 0%

commit v1 on v0

--- a/solution.py
+++ b/solution.py
@@ -4,6 +4,7 @@
 from jax import lax
 from jax.sharding import Mesh
 from jax.sharding import PartitionSpec as P
+from jax.lax import all_to_all, psum
 
 WINDOW = 32
 TOK_VOC = ("tok_0", "tok_1", "voc_0", "voc_1")
@@ -20,7 +21,11 @@
 def gather_in_order(value, axes, turns):
     parts = value[None]
     for k in turns:
-        parts = lax.all_gather(parts, axes[k], axis=0, tiled=True)
+        x0 = axes[k]
+        samples = []
+        for _ in range(psum(1, x0)):
+            samples.append(parts)
+        parts = jnp.concatenate(all_to_all(jnp.stack(samples, axis=0), x0, 0, 0), axis=0)
     held = [lax.axis_size(axes[k]) for k in reversed(turns)]
     parts = parts.reshape(*held, *value.shape)
     turned = sorted(range(len(turns)), key=lambda place: turns[len(turns) - 1 - place])

time: 210 us -> 186 us (0.89)
  waiting for transfers between devices: 96.3 us -> 49.7 us
  blocking collectives: 80.2 us -> 103 us
    all_to_all x0 -> x2, blocking collectives: none -> 56.2 us  [gather_in_order(): all_to_all(jnp.stack(samples, axis=0), x0, 0, 0)]
    all_gather x1 -> x0, waiting for transfers between devices: 39.3 us -> none  [gather_in_order(): parts = lax.all_gather(parts, axes[k], axis=0, tiled=True)]
    all_gather x1 -> x0, blocking collectives: 33 us -> none  [gather_in_order(): parts = lax.all_gather(parts, axes[k], axis=0, tiled=True)]
    all_gather x1, waiting for transfers between devices: 56.9 us -> 49.7 us  [body(): lax.all_gather(grouped, TOK, axis=0, tiled=True)]
  transfers between devices with their start and end apart: 2 -> 1, of which waited for: 2 -> 1; matrix products, arithmetic and copies ran while one was open for 0% -> 1% of each run, Pallas kernels for 0% -> 0%
where the time goes in v1:
time: 186 us
  blocking collectives  103 us (55%)
  waiting for transfers between devices  49.7 us (27%)
  between operations  16.6 us (9%)
  matrix products  9.46 us (5%)
  local copies, waits for them, and re-layouts  3.55 us (2%)
  other arithmetic  3.11 us (2%)
    all_to_all x2, blocking collectives, gather_in_order(): all_to_all(jnp.stack(samples, axis=0), x0, 0, 0)  56.2 us
    all_gather x1, waiting for transfers between devices, body(): lax.all_gather(grouped, TOK, axis=0, tiled=True)  49.7 us
    psum x4, blocking collectives, over_axes(): return functools.reduce(lax.psum, axes, value)  47.2 us
    dot_general x1, matrix products, body(): lax.dot_general(lax.all_gather(grouped, TOK, axis=0, tiled=True), head_we...  9.46 us
  transfers between devices with their start and end apart: 1, of which 1 were waited for; matrix products, arithmetic and copies ran while one was open for 1% of the time, Pallas kernels for 0%

profile of v1, /device:TPU:2, one launch (start us, length us, event | category | flops | bytes accessed | tf_op | source)
XLA Modules:
  0.0 185.9 jit_solution(18204719648632586857)
XLA Ops:
  7.2 0.0 all-gather.2.cloned.1.call-start
  7.2 0.9 fusion
  8.1 0.8 fusion.2
  8.9 0.1 stack.15
  9.0 19.5 %all_to_all.10 = bf16[8,1,2,4608]{3,2,1,0:T(2,128)(2,1)S(1)} all-to-all(bf16[8,1,2,4608]{3,2,1,0:T(2,128)(2,1)S(1)} %stack.15), channel_id=1, replica_groups=mesh['tok_0'=4,'tok_1'=2,'voc_0'=8,'voc_1'=8] {'voc_0'}, dimensions={0} | all-to-all | bytes 294912 | tf_op jit(solution)/shard_map/all_to_all | solution.py:28
  28.6 0.6 stack.16
  29.2 36.6 %all_to_all.11 = bf16[8,8,2,4608]{3,2,1,0:T(2,128)(2,1)S(1)} all-to-all(bf16[8,8,2,4608]{3,2,1,0:T(2,128)(2,1)S(1)} %stack.16), channel_id=1, replica_groups=mesh['tok_0'=4,'tok_1'=2,'voc_0'=8,'voc_1'=8] {'voc_1'}, dimensions={0} | all-to-all | bytes 2359296 | tf_op jit(solution)/shard_map/all_to_all | solution.py:28
  65.8 0.8 copy.8
  66.6 0.0 copy-start.1
  66.6 0.0 copy-start
  66.7 1.3 reshape_reshape.3
  67.9 0.0 all-gather.2.cloned.1.call-update
  68.0 0.1 iota_compare_fusion.1
  68.0 0.1 lt.34
  68.1 0.1 lt.32
  68.2 0.7 convert_reduce_fusion
  68.9 49.7 %all-gather.2.cloned.1.call-done = bf16[1024,4608]{1,0:T(8,128)(2,1)} async-done(((bf16[128,4608]{1,0:T(8,128)(2,1)}), bf16[1024,4608]{1,0:T(8,128)(2,1)}) %all-gather.2.cloned.1.call-update) | async-done | bytes 9437200 | tf_op jit(solution)/shard_map/all_gather | solution.py:57
  118.6 9.5 %exponential_reduce_fusion = (f32[1024]{0:T(1024)S(1)}, f32[1024]{0:T(1024)S(1)}) fusion(s32[1024]{0:T(1024)S(1)} %broadcast_subtract_fusion, bf16[1024,4608]{1,0:T(8,128)(2,1)} %all-gather.2.cloned.1.call-done, bf16[512,4608]{1,0:T(8,128)(2,1)} %param.7), kind=kOutput, calls=%fused_computation.2 | convolution fusion | flops 4834981888 | bytes 14168064 | tf_op jit(solution)/shard_map/dot_general | solution.py:56
  128.1 9.1 %psum.28 = f32[2,1024]{1,0:T(2,128)S(1)} all-reduce(f32[2,1024]{1,0:T(2,128)S(1)} %pad_maximum_fusion), channel_id=1, replica_groups=mesh['tok_0'=4,'tok_1'=2,'voc_0'=8,'voc_1'=8] {'tok_0'}, use_global_device_ids=true, to_apply=%region_3.4 | all-reduce | flops 2048 | bytes 16384 | tf_op jit(solution)/shard_map/psum | solution.py:40
  137.2 2.5 %psum.29 = f32[2,1024]{1,0:T(2,128)S(1)} all-reduce(f32[2,1024]{1,0:T(2,128)S(1)} %psum.28), channel_id=1, replica_groups=mesh['tok_0'=4,'tok_1'=2,'voc_0'=8,'voc_1'=8] {'tok_1'}, use_global_device_ids=true, to_apply=%region_4.5 | all-reduce | flops 2048 | bytes 16384 | tf_op jit(solution)/shard_map/psum | solution.py:40
  139.7 18.3 %psum.30 = f32[2,1024]{1,0:T(2,128)S(1)} all-reduce(f32[2,1024]{1,0:T(2,128)S(1)} %psum.29), channel_id=1, replica_groups=mesh['tok_0'=4,'tok_1'=2,'voc_0'=8,'voc_1'=8] {'voc_0'}, use_global_device_ids=true, to_apply=%region_5.6 | all-reduce | flops 2048 | bytes 16384 | tf_op jit(solution)/shard_map/psum | solution.py:40
  158.1 17.2 %psum.31 = f32[2,1024]{1,0:T(2,128)S(1)} all-reduce(f32[2,1024]{1,0:T(2,128)S(1)} %psum.30), channel_id=1, replica_groups=mesh['tok_0'=4,'tok_1'=2,'voc_0'=8,'voc_1'=8] {'voc_1'}, use_global_device_ids=true, to_apply=%region_6.7 | all-reduce | flops 2048 | bytes 16384 | tf_op jit(solution)/shard_map/psum | solution.py:40
  175.3 0.6 select_reduce_fusion.1
  175.9 0.6 dynamic_slice.3
  (6 shorter events, 0.0 us)
Async XLA Ops:
  7.2 111.5 %all-gather.2.cloned.1.call-start = ((), (), s32[]{:S(2)}) async-start(), calls=%async_computation.2 | async-start | bytes 10616832 | tf_op jit(solution)/shard_map/all_gather | solution.py:57
  66.6 1.3 copy-start.1
  66.6 2.3 %copy-start = (s32[1024]{0:T(1024)S(1)}, s32[1024]{0:T(1024)}, u32[]{:S(2)}) copy-start(s32[1024]{0:T(1024)} %param.8) | copy-start | bytes 12292
Sparse Core Ops, SparseCore 0:
  68.1 50.4 all-gather.1
